TPU v7x, 32 devices: a whole 2x2x4 slice. The times are simulated.
32 devices in a mesh: groups: 2 (over y), bank: 4 (over x, core), tensor: 4 (over z).
Axes of the slice: x: 2, y: 2, z: 4, core: 2. Of those that a mesh axis runs over, the one named last changes fastest.
Arguments:
- latest_activations: bfloat16 [64, 8192], P(('groups', 'bank'), 'tensor'), parts along dimension 0, may hold values from -6 to 6
- layer_normalizer_gains_table: bfloat16 [8192], replicated, may hold values from 0.5 to 1.5
- asker_projection: bfloat16 [8192, 8192], P('bank', 'tensor'), may hold values from -0.0625 to 0.0625
- memory_projection_stack: bfloat16 [2, 8192, 1024], P(None, 'bank', 'tensor'), may hold values from -0.0625 to 0.0625
- narrowing_factors: bfloat16 [128, 48, 8192], P('bank', None, 'tensor'), may hold values from -0.0625 to 0.0625
- widening_factors_asker: bfloat16 [128, 16, 8192], P('bank', None, 'tensor'), may hold values from -1.5 to 1.5
- widening_factors_memory: bfloat16 [128, 2, 16, 1024], P('bank', None, None, 'tensor'), may hold values from -1.5 to 1.5
- tweak_for_stream: int32 [64], P(('groups', 'bank')), parts along dimension 0, may hold values from 0 to 127
- stream_offsets: int32 [64], P(('groups', 'bank')), parts along dimension 0, may hold values from 2 to 1024
- saved_rotated_addresses: bfloat16 [64, 1024, 8, 128], P(('groups', 'bank'), None, 'tensor'), parts along dimension 0, may hold values from -1200 to 1200
- saved_contents: bfloat16 [64, 1024, 8, 128], P(('groups', 'bank'), None, 'tensor'), parts along dimension 0, may hold values from -6 to 6
Outputs:
- attention: bfloat16 [64, 8192], P(('groups', 'bank'), 'tensor'), parts along dimension 0
There are 2 independent parts, one for each index of `groups`. A program takes and returns all parts, laid end to end along the dimension named above; an argument that names none is the same for every part. Nothing has to cross between parts.
All inputs are finite; a program needn't handle non-finite values.
Results may differ from a plain program's by a relative error of at most 0.0095.
The roundings to bfloat16 on the way count: a program that leaves them out, or rounds other values in their place, can miss the bound.
Values may be sent and summed in bfloat16 or wider, within the bound.
No kernel may reach another device: no remote copies, remote signals or barrier semaphores. Data moves between devices by JAX's collectives and lax.ppermute only.
A program may use at most 64 MiB of HBM per device.

v0:
```python
import math
import jax
import jax.numpy as jnp
from jax import lax
from jax.sharding import PartitionSpec as P

rope_base = 500000.0
tweak_strength = 2.0
epsilon = 1e-05


def rotate(values, positions):
    half_dim = values.shape[-1] // 2
    freqs = rope_base ** (-(jnp.arange(half_dim, dtype=jnp.float32) * 2.0) / values.shape[-1])
    angles = positions.astype(jnp.float32)[:, None] * freqs[None, :]
    cosine = jnp.cos(angles)[:, None, :]
    sine_part = jnp.sin(angles)[:, None, :]
    front_half = values[..., :half_dim]
    back_half = values[..., half_dim:]
    return jnp.concatenate(
        [front_half * cosine - back_half * sine_part, back_half * cosine + front_half * sine_part],
        axis=-1,
    )


def attend_local(
    probe_vectors, current_lookup_vectors, values_new, cache_keys, cache_values, stream_offsets
):
    reciprocal_sqrt_dim = 1.0 / math.sqrt(probe_vectors.shape[-1])
    scores = (
        jnp.einsum("bkgd,bpkd->bkgp", probe_vectors, cache_keys, preferred_element_type=jnp.float32)
        * reciprocal_sqrt_dim
    )
    self_logit = (
        jnp.einsum(
            "atcj,atj->atc",
            probe_vectors,
            current_lookup_vectors,
            preferred_element_type=jnp.float32,
        )
        * reciprocal_sqrt_dim
    )
    positions = lax.broadcasted_iota(jnp.int32, scores.shape, 3)
    live_mask = positions < stream_offsets[:, None, None, None]
    peak_score = jnp.maximum(jnp.max(jnp.where(live_mask, scores, -jnp.inf), axis=-1), self_logit)
    expo = jnp.where(live_mask, jnp.exp(scores - peak_score[..., None]), 0.0)
    own_expo = jnp.exp(self_logit - peak_score)
    total = jnp.sum(expo, axis=-1) + own_expo
    weights = (expo / total[..., None]).astype(jnp.bfloat16)
    own_weight = (own_expo / total).astype(jnp.bfloat16)
    mixed = jnp.einsum("bkgp,bpkd->bkgd", weights, cache_values, preferred_element_type=jnp.float32)
    return (
        mixed
        + own_weight.astype(jnp.float32)[..., None] * values_new.astype(jnp.float32)[:, :, None, :]
    )


def shards(
    latest_activations,
    layer_normalizer_gains_table,
    asker_projection,
    memory_projection_stack,
    narrowing_factors,
    widening_factors_asker,
    widening_factors_memory,
    tweak_for_stream,
    stream_offsets,
    saved_rotated_addresses,
    saved_contents,
):
    joined_rows = lax.all_gather(latest_activations, "tensor", axis=1, tiled=True)
    tok_float = joined_rows.astype(jnp.float32)
    mean_square = jnp.mean(tok_float * tok_float, axis=1, keepdims=True)
    normed = (
        tok_float
        * lax.rsqrt(mean_square + epsilon)
        * layer_normalizer_gains_table.astype(jnp.float32)[None, :]
    ).astype(jnp.bfloat16)
    n_bank = lax.axis_size("bank")
    n_tensor = lax.axis_size("tensor")
    bank_index = lax.axis_index("bank")
    tensor_index = lax.axis_index("tensor")
    model_width = normed.shape[1]
    piece_bank = model_width // n_bank
    piece_tensor = model_width // n_tensor
    row_count = latest_activations.shape[0]
    every_row, all_ids = (
        lax.all_gather(normed, "bank", axis=0, tiled=True),
        lax.all_gather(tweak_for_stream, "bank", axis=0, tiled=True),
    )
    base_input = lax.dynamic_slice_in_dim(every_row, bank_index * piece_bank, piece_bank, 1)
    hidden_after_rmsnorm = lax.dynamic_slice_in_dim(
        every_row, tensor_index * piece_tensor, piece_tensor, 1
    )
    sequences_on_device = narrowing_factors.shape[0]
    low_dim_extent = widening_factors_asker.shape[1]
    owned_ids = bank_index * sequences_on_device + jnp.arange(sequences_on_device, dtype=jnp.int32)
    picked = all_ids[None, :] == owned_ids[:, None]
    projected_low_vector = jnp.einsum(
        "omk,lk->oml", narrowing_factors, hidden_after_rmsnorm, preferred_element_type=jnp.float32
    )
    inner_part = jnp.sum(jnp.where(picked[:, None, :], projected_low_vector, 0.0), axis=0)
    inner_sum = lax.psum(inner_part, "tensor")
    inner_low = inner_sum.astype(jnp.bfloat16)
    pick_low = picked.astype(jnp.bfloat16)

    def spread(rank_block):
        expanded = pick_low[:, None, :] * rank_block[None, :, :]
        return expanded.reshape(sequences_on_device * low_dim_extent, rank_block.shape[1])

    probe_proj_span = asker_projection.shape[1]
    shared_proj_span = memory_projection_stack.shape[2]
    probe_correction = jnp.einsum(
        "cs,co->so",
        spread(inner_low[0:low_dim_extent]),
        widening_factors_asker.reshape(sequences_on_device * low_dim_extent, probe_proj_span),
        preferred_element_type=jnp.float32,
    )
    lookup_correction = jnp.einsum(
        "cs,co->so",
        spread(inner_low[low_dim_extent : 2 * low_dim_extent]),
        widening_factors_memory[:, 0].reshape(
            sequences_on_device * low_dim_extent, shared_proj_span
        ),
        preferred_element_type=jnp.float32,
    )
    payload_correction = jnp.einsum(
        "cs,co->so",
        spread(inner_low[2 * low_dim_extent : 3 * low_dim_extent]),
        widening_factors_memory[:, 1].reshape(
            sequences_on_device * low_dim_extent, shared_proj_span
        ),
        preferred_element_type=jnp.float32,
    )
    tweak_contribution = tweak_strength * jnp.concatenate(
        [probe_correction, lookup_correction, payload_correction], axis=1
    )
    untouched_share = lax.psum_scatter(
        jnp.concatenate(
            [
                jnp.dot(base_input, asker_projection, preferred_element_type=jnp.float32),
                jnp.dot(base_input, memory_projection_stack[0], preferred_element_type=jnp.float32),
                jnp.dot(base_input, memory_projection_stack[1], preferred_element_type=jnp.float32),
            ],
            axis=1,
        ),
        "bank",
        scatter_dimension=0,
        tiled=True,
    )
    accumulated_total = untouched_share + lax.psum_scatter(
        tweak_contribution, "bank", scatter_dimension=0, tiled=True
    )
    head_dim = saved_rotated_addresses.shape[3]
    kv_heads = saved_rotated_addresses.shape[2]
    q_heads = probe_proj_span // head_dim
    query_part = accumulated_total[:, 0:probe_proj_span].reshape(row_count, q_heads, head_dim)
    key_part = accumulated_total[:, probe_proj_span : probe_proj_span + shared_proj_span].reshape(
        row_count, kv_heads, head_dim
    )
    value_part = accumulated_total[
        :, probe_proj_span + shared_proj_span : probe_proj_span + 2 * shared_proj_span
    ].reshape(row_count, kv_heads, head_dim)
    q_rot = rotate(query_part, stream_offsets).astype(jnp.bfloat16)
    k_new = rotate(key_part, stream_offsets).astype(jnp.bfloat16)
    v_new = value_part.astype(jnp.bfloat16)
    probe_vectors = q_rot.reshape(row_count, kv_heads, q_heads // kv_heads, head_dim)
    mixed = attend_local(
        probe_vectors, k_new, v_new, saved_rotated_addresses, saved_contents, stream_offsets
    )
    return mixed.reshape(row_count, probe_proj_span).astype(jnp.bfloat16)


def solution(mesh):
    placed = (
        P(("groups", "bank"), "tensor"),
        P(),
        P("bank", "tensor"),
        P(None, "bank", "tensor"),
        P("bank", None, "tensor"),
        P("bank", None, "tensor"),
        P("bank", None, None, "tensor"),
        P(("groups", "bank")),
        P(("groups", "bank")),
        P(("groups", "bank"), None, "tensor", None),
        P(("groups", "bank"), None, "tensor", None),
    )
    return jax.shard_map(
        shards,
        mesh=mesh,
        in_specs=placed,
        out_specs=P(("groups", "bank"), "tensor"),
        check_vma=False,
    )
```

profile of v0, /device:TPU:0, one launch (start us, length us, event | category | flops | bytes accessed | tf_op | source)
XLA Modules:
  0.0 105.4 jit_solution(16486017365840379025)
XLA Ops:
  6.5 0.0 copy-start
  6.5 0.0 reduce-scatter.2.cloned.1.call-start
  6.5 15.4 %all_gather.9 = bf16[8,8192]{1,0:T(8,128)(2,1)S(1)} all-gather(bf16[8,2048]{1,0:T(8,128)(2,1)} %param.11), channel_id=1, replica_groups=mesh['groups'=2,'bank'=4,'tensor'=4] {'tensor'}, dimensions={1}, use_global_device_ids=true | all-gather | bytes 163840 | tf_op jit(solution)/shard_map/all_gather | solution.py:71
  22.0 0.7 convert_element_type.58
  22.7 0.2 fusion.25
  22.9 0.1 fusion.27
  23.0 7.2 %all_gather.10 = bf16[32,8192]{1,0:T(8,128)(2,1)S(1)} all-gather(bf16[8,8192]{1,0:T(8,128)(2,1)S(1)} %fusion.27), channel_id=1, replica_groups=mesh['groups'=2,'bank'=4,'tensor'=4] {'bank'}, dimensions={0}, use_global_device_ids=true | all-gather | bytes 655360 | tf_op jit(solution)/shard_map/all_gather | solution.py:88
  30.2 1.5 %fusion.18 = f32[32,256]{1,0:T(8,128)S(1)} fusion(bf16[2,2048,256]{2,1,0:T(8,128)(2,1)} %param.14, bf16[32,8192]{1,0:T(8,128)(2,1)S(1)} %all_gather.10, s32[]{:T(128)S(6)} %select_n.17), kind=kOutput, calls=%fused_computation.12 | convolution fusion | flops 33554432 | bytes 1212420 | tf_op jit(solution)/shard_map/dot_general | solution.py:143
  31.7 1.5 %fusion.20 = f32[32,256]{1,0:T(8,128)S(1)} fusion(bf16[2,2048,256]{2,1,0:T(8,128)(2,1)} %param.14, bf16[32,8192]{1,0:T(8,128)(2,1)S(1)} %all_gather.10, s32[]{:T(128)S(6)} %select_n.17), kind=kOutput, calls=%fused_computation.14 | convolution fusion | flops 33554432 | bytes 1212420 | tf_op jit(solution)/shard_map/dot_general | solution.py:142
  33.2 0.0 copy-start.5
  33.2 0.0 copy-start.4
  33.2 4.9 %fusion.37 = f32[32,2048]{1,0:T(8,128)S(1)} fusion(bf16[2048,2048]{1,0:T(8,128)(2,1)} %param.13, bf16[32,8192]{1,0:T(8,128)(2,1)S(1)} %all_gather.10, s32[]{:T(128)S(6)} %select_n.17), kind=kOutput, calls=%fused_computation.39 | convolution fusion | flops 268435456 | bytes 8781828 | tf_op jit(solution)/shard_map/dot_general | solution.py:141
  38.1 0.0 copy-start.1
  38.2 0.0 copy-done.5
  38.2 0.6 dynamic-slice
  39.4 0.0 copy-done.4
  39.4 0.2 dynamic-update-slice
  39.7 4.3 %all-reduce = s32[32]{0:T(128)S(1)} all-reduce(s32[32]{0:T(128)S(1)} %dynamic-update-slice), channel_id=1, replica_groups=mesh['groups'=2,'bank'=4,'tensor'=4] {'bank'}, use_global_device_ids=true, to_apply=%add | all-reduce | flops 32 | bytes 256
  43.9 0.1 fusion.54
  44.0 6.5 %fusion.8 = f32[48,32]{0,1:T(8,128)S(1)} fusion(bf16[32,48,2048]{2,1,0:T(8,128)(2,1)} %param.15, pred[32,32]{1,0:T(8,128)(4,1)S(1)} %get-tuple-element.21, bf16[32,8192]{1,0:T(8,128)(2,1)S(1)} %all_gather.10, s32[]{:T(128)S(6)} %select_n.18), kind=kOutput, calls=%fused_computation.8 | convolution fusion | flops 201423360 | bytes 6432772 | tf_op jit(solution)/shard_map/omk,lk->oml/dot_general | solution.py:99
  50.5 0.0 copy-start.2
  50.5 19.1 %psum.7 = bf16[48,32]{0,1:T(8,128)(2,1)S(1)} all-reduce(f32[48,32]{0,1:T(8,128)S(1)} %fusion.8), channel_id=1, replica_groups=mesh['groups'=2,'bank'=4,'tensor'=4] {'tensor'}, use_global_device_ids=true, to_apply=%region_3.4 | all-reduce | flops 1536 | bytes 9216 | tf_op jit(solution)/shard_map/psum | solution.py:103
  69.6 0.1 fusion.56
  69.7 0.1 copy.27
  69.8 0.1 copy.28
  69.9 0.0 copy-done.1
  69.9 0.1 copy.26
  70.0 0.2 fusion.58
  70.2 0.2 fusion.57
  70.4 0.0 copy-done
  70.4 0.5 convolution_bitcast_fusion
  70.9 0.8 maximum_add_fusion
  71.7 0.0 reduce-scatter.2.cloned.1.call-update
  71.7 0.0 copy-done.2
  71.7 0.1 multiply_cosine_fusion
  71.8 18.3 %reduce-scatter.2.cloned.1.call-done = f32[8,2560]{1,0:T(8,128)} async-done(((f32[32,2560]{1,0:T(8,128)}), f32[8,2560]{1,0:T(8,128)}) %reduce-scatter.2.cloned.1.call-update) | async-done | bytes 81936 | tf_op jit(solution)/shard_map/reduce_scatter | solution.py:138
  90.2 0.0 copy-start.3
  90.2 1.0 slice_bitcast_fusion
  91.2 0.1 subtract_convert_fusion
  91.3 0.9 slice_bitcast_fusion.1
  92.2 0.1 subtract_convert_fusion.1
  92.3 0.1 maximum_bitcast_fusion
  92.4 3.5 %select_reduce_fusion = (f32[8,2,8]{2,1,0:T(2,128)S(1)}, f32[8,2,8,1024]{3,2,1,0:T(8,128)S(1)}) fusion(s32[8]{0:T(128)S(1)} %copy-done.2, bf16[8,1024,2,128]{3,2,1,0:T(2,128)(2,1)} %param.20, bf16[8,2,8,64]{3,2,1,0:T(8,128)(2,1)S(1)} %get-tuple-element.24, bf16[8,2,8,64]{3,2,1,0:T(8,128)(2,1)S(1)} %get-tuple-element.25), kind=kOutput, calls=%fused_computation.20 | convolution fusion | flops 34144128 | bytes 4751904 | tf_op jit(solution)/shard_map/bkgd,bpkd->bkgp/dot_general | solution.py:31
  95.9 0.2 fusion.41
  96.1 0.3 fusion.24
  96.4 0.7 fusion.44
  97.1 0.0 copy-done.3
  97.1 0.8 fusion.15
  97.9 0.6 copy.56
  (11 shorter events, 0.2 us)
Async XLA Ops:
  6.5 63.9 %copy-start = (bf16[32,16,2048]{2,1,0:T(8,128)(2,1)S(1)}, bf16[32,16,2048]{2,1,0:T(8,128)(2,1)}, u32[]{:S(2)}) copy-start(bf16[32,16,2048]{2,1,0:T(8,128)(2,1)} %param.16) | copy-start | bytes 6291460
  6.5 83.7 %reduce-scatter.2.cloned.1.call-start = ((), (), s32[]{:S(2)}) async-start(), calls=%async_computation.1 | async-start | bytes 409600 | tf_op jit(solution)/shard_map/reduce_scatter | solution.py:138
  33.2 5.0 %copy-start.5 = (u32[32]{0:T(128)S(1)}, u32[32]{0:T(128)}, u32[]{:S(2)}) copy-start(u32[32]{0:T(128)} %constant.39) | copy-start | bytes 388
  33.2 6.2 %copy-start.4 = (s32[8]{0:T(128)S(1)}, s32[8]{0:T(128)}, u32[]{:S(2)}) copy-start(s32[8]{0:T(128)} %param.18) | copy-start | bytes 100
  38.1 31.7 %copy-start.1 = (bf16[32,2,16,256]{3,2,1,0:T(8,128)(2,1)S(1)}, bf16[32,2,16,256]{3,2,1,0:T(8,128)(2,1)}, u32[]{:S(2)}) copy-start(bf16[32,2,16,256]{3,2,1,0:T(8,128)(2,1)} %param.17) | copy-start | bytes 1572868
  50.5 21.2 %copy-start.2 = (s32[8]{0:T(128)S(1)}, s32[8]{0:T(128)}, u32[]{:S(2)}) copy-start(s32[8]{0:T(128)} %param.19) | copy-start | bytes 100
  90.2 6.9 %copy-start.3 = (bf16[8,1024,2,128]{3,2,1,0:T(2,128)(2,1)S(1)}, bf16[8,1024,2,128]{3,2,1,0:T(2,128)(2,1)}, u32[]{:S(2)}) copy-start(bf16[8,1024,2,128]{3,2,1,0:T(2,128)(2,1)} %param.21) | copy-start | bytes 12582916
Sparse Core Ops, SparseCore 0:
  71.8 18.3 reduce-scatter.1
where the time goes:
time: 106 us; the launch traced here: 105 us
  blocking collectives  46 us (43%)
  matrix products  19.8 us (19%)
  waiting for transfers between devices  18.4 us (17%)
  between operations  14.2 us (13%)
  local copies, waits for them, and re-layouts  3.78 us (4%)
  other arithmetic  3.25 us (3%)
    psum x1, blocking collectives, shards(): inner_sum = lax.psum(inner_part, 'tensor')  19.1 us
    reduce_scatter x1, waiting for transfers between devices, shards(): lax.psum_scatter(jnp.concatenate([jnp.dot(base_input, asker_projection, p...  18.3 us
    all_gather x1, blocking collectives, shards(): lax.all_gather(latest_activations, 'tensor', axis=1, tiled=True)  15.4 us
    all_gather x1, blocking collectives, shards(): lax.all_gather(normed, 'bank', axis=0, tiled=True)  7.17 us
    dot_general x1, matrix products, shards(): jnp.einsum('omk,lk->oml', narrowing_factors, hidden_after_rmsnorm, prefer...  6.49 us
    dot_general x1, matrix products, shards(): jnp.dot(base_input, asker_projection, preferred_element_type=jnp.float32)  4.93 us
    unnamed x1, blocking collectives  4.26 us
    dot_general x1, matrix products, attend_local(): jnp.einsum('bkgd,bpkd->bkgp', probe_vectors, cache_keys, preferred_elemen...  3.5 us
  transfers between devices with their start and end apart: 1, of which 1 were waited for; matrix products, arithmetic and copies ran while one was open for 0% of the time, Pallas kernels for 0%

commit v1 on v0

--- a/solution.py
+++ b/solution.py
@@ -68,7 +68,14 @@
     saved_rotated_addresses,
     saved_contents,
 ):
-    joined_rows = lax.all_gather(latest_activations, "tensor", axis=1, tiled=True)
+    ring = [latest_activations]
+    for hop in range(3):
+        ring.append(lax.ppermute(ring[-1], "tensor", [(dev, (dev + 1) % 4) for dev in range(4)]))
+    joined_rows = jnp.roll(
+        jnp.concatenate(ring[::-1], axis=1),
+        (lax.axis_index("tensor") + 1) * ring[0].shape[1],
+        axis=1,
+    )
     tok_float = joined_rows.astype(jnp.float32)
     mean_square = jnp.mean(tok_float * tok_float, axis=1, keepdims=True)
     normed = (

time: 106 us -> 101 us (0.953)
  blocking collectives: 46 us -> 29.1 us
  waiting for transfers between devices: 18.4 us -> 24.9 us
  starting transfers between devices: 0.01 us -> 4.41 us
  local copies, waits for them, and re-layouts: 3.78 us -> 7.64 us
  matrix products: 19.8 us -> 17.3 us
    all_gather x1 -> x0, blocking collectives: 15.4 us -> none  [shards(): lax.all_gather(latest_activations, 'tensor', axis=1, tiled=True)]
    ppermute x0 -> x3, waiting for transfers between devices: none -> 6.61 us  [shards(): lax.ppermute(ring[-1], 'tensor', [(dev, (dev + 1) % 4) for dev in range(4)])]
    ppermute x0 -> x3, starting transfers between devices: none -> 4.41 us  [shards(): lax.ppermute(ring[-1], 'tensor', [(dev, (dev + 1) % 4) for dev in range(4)])]
    dot_general x1, matrix products: 6.49 us -> 3.71 us  [shards(): jnp.einsum('omk,lk->oml', narrowing_factors, hidden_after_rmsnorm, prefer...]
    unnamed x16 -> x21, local copies, waits for them, and re-layouts: 1.5 us -> 3.56 us
    psum x1, blocking collectives: 19.1 us -> 17.4 us  [shards(): inner_sum = lax.psum(inner_part, 'tensor')]
  transfers between devices with their start and end apart: 1 -> 4, of which waited for: 1 -> 3; matrix products, arithmetic and copies ran while one was open for 0% -> 4% of each run, Pallas kernels for 0% -> 0%
where the time goes in v1:
time: 101 us
  blocking collectives  29.1 us (29%)
  waiting for transfers between devices  24.9 us (25%)
  matrix products  17.3 us (17%)
  between operations  14.2 us (14%)
  local copies, waits for them, and re-layouts  7.64 us (8%)
  starting transfers between devices  4.41 us (4%)
  other arithmetic  3.24 us (3%)
    reduce_scatter x1, waiting for transfers between devices, shards(): lax.psum_scatter(jnp.concatenate([jnp.dot(base_input, asker_projection, p...  18.3 us
    psum x1, blocking collectives, shards(): inner_sum = lax.psum(inner_part, 'tensor')  17.4 us
    ppermute x3, waiting for transfers between devices, shards(): lax.ppermute(ring[-1], 'tensor', [(dev, (dev + 1) % 4) for dev in range(4)])  6.61 us
    all_gather x1, blocking collectives, shards(): lax.all_gather(normed, 'bank', axis=0, tiled=True)  6.58 us
    unnamed x1, blocking collectives  5.12 us
    dot_general x1, matrix products, shards(): jnp.dot(base_input, asker_projection, preferred_element_type=jnp.float32)  5.08 us
    ppermute x3, starting transfers between devices, shards(): lax.ppermute(ring[-1], 'tensor', [(dev, (dev + 1) % 4) for dev in range(4)])  4.41 us
    dot_general x1, matrix products, shards(): jnp.einsum('omk,lk->oml', narrowing_factors, hidden_after_rmsnorm, prefer...  3.71 us
  transfers between devices with their start and end apart: 4, of which 3 were waited for; matrix products, arithmetic and copies ran while one was open for 4% of the time, Pallas kernels for 0%

profile of v1, /device:TPU:0, one launch (start us, length us, event | category | flops | bytes accessed | tf_op | source)
XLA Modules:
  0.0 100.9 jit_solution(4204477252706438824)
XLA Ops:
  6.5 0.0 copy-start
  6.5 0.0 reduce-scatter.2.cloned.1.call-start
  6.5 3.1 %collective-permute-start = (bf16[8,2048]{1,0:T(8,128)(2,1)}, bf16[8,2048]{1,0:T(8,128)(2,1)S(1)}, u32[]{:S(2)}, u32[]{:S(2)}) collective-permute-start(bf16[8,2048]{1,0:T(8,128)(2,1)} %param.11), channel_id=1, source_target_pairs={{0,1},{1,2},{2,3},{3,0},{4,5},{5,6},{6,7},{7,4},{8,9},{9,10},{10,1... | collective-permute-start | bytes 98312 | tf_op jit(solution)/shard_map/ppermute | solution.py:73
  9.6 1.1 %fusion.55 = (bf16[32,1,16,256]{3,2,1,0:T(8,128)(2,1)S(1)}, bf16[32,1,16,256]{3,2,1,0:T(8,128)(2,1)S(1)}) fusion(bf16[32,2,16,256]{3,2,1,0:T(8,128)(2,1)} %param.17), kind=kLoop, calls=%fused_computation.88 | loop fusion | bytes 1048576 | tf_op jit(solution)/shard_map/slice | solution.py:129
  10.7 3.0 %collective-permute-done = bf16[8,2048]{1,0:T(8,128)(2,1)S(1)} collective-permute-done((bf16[8,2048]{1,0:T(8,128)(2,1)}, bf16[8,2048]{1,0:T(8,128)(2,1)S(1)}, u32[]{:S(2)}, u32[]{:S(2)}) %collective-permute-start) | collective-permute-done | bytes 32800 | tf_op jit(solution)/shard_map/ppermute | solution.py:73
  13.7 0.0 collective-permute-start.1
  13.7 1.2 %dynamic-slice = u32[1]{0:T(128)} dynamic-slice(u32[32]{0:T(128)} %constant.61, u32[]{:T(128)S(6)} %add.72), dynamic_slice_sizes={1} | dynamic-slice | bytes 12
  15.6 0.9 dynamic-update-slice
  16.5 5.1 %all-reduce = s32[32]{0:T(128)S(1)} all-reduce(s32[32]{0:T(128)S(1)} %dynamic-update-slice), channel_id=1, replica_groups=mesh['groups'=2,'bank'=4,'tensor'=4] {'bank'}, use_global_device_ids=true, to_apply=%add | all-reduce | flops 32 | bytes 256
  21.6 0.0 collective-permute-done.1
  21.6 1.4 %collective-permute-start.2 = (bf16[8,2048]{1,0:T(8,128)(2,1)S(1)}, bf16[8,2048]{1,0:T(8,128)(2,1)S(1)}, u32[]{:S(2)}, u32[]{:S(2)}) collective-permute-start(bf16[8,2048]{1,0:T(8,128)(2,1)S(1)} %collective-permute-done.1), channel_id=1, source_target_pairs={{0,1},{1,2},{2,3},{3,0},{4,5},{5,6},{6,7},{7,4},{8,9},{9,10},{10,1... | collective-permute-start | bytes 98312 | tf_op jit(solution)/shard_map/ppermute | solution.py:73
  23.0 0.1 fusion.54
  23.0 0.7 convert_element_type.58
  23.8 3.6 %collective-permute-done.2 = bf16[8,2048]{1,0:T(8,128)(2,1)S(1)} collective-permute-done((bf16[8,2048]{1,0:T(8,128)(2,1)S(1)}, bf16[8,2048]{1,0:T(8,128)(2,1)S(1)}, u32[]{:S(2)}, u32[]{:S(2)}) %collective-permute-start.2) | collective-permute-done | bytes 32800 | tf_op jit(solution)/shard_map/ppermute | solution.py:73
  27.3 0.8 constant_dynamic-update-slice_fusion.4
  28.1 0.8 constant_dynamic-update-slice_fusion
  28.9 0.2 fusion.25
  29.1 0.1 fusion.27
  29.2 6.6 %all_gather.6 = bf16[32,8192]{1,0:T(8,128)(2,1)S(1)} all-gather(bf16[8,8192]{1,0:T(8,128)(2,1)S(1)} %fusion.27), channel_id=1, replica_groups=mesh['groups'=2,'bank'=4,'tensor'=4] {'bank'}, dimensions={0}, use_global_device_ids=true | all-gather | bytes 655360 | tf_op jit(solution)/shard_map/all_gather | solution.py:95
  35.8 1.5 %fusion.18 = f32[32,256]{1,0:T(8,128)S(1)} fusion(bf16[2,2048,256]{2,1,0:T(8,128)(2,1)} %param.14, bf16[32,8192]{1,0:T(8,128)(2,1)S(1)} %all_gather.6, s32[]{:T(128)S(6)} %select_n.32), kind=kOutput, calls=%fused_computation.12 | convolution fusion | flops 33554432 | bytes 1212420 | tf_op jit(solution)/shard_map/dot_general | solution.py:150
  37.3 0.0 slice-start
  37.3 1.7 %fusion.20 = f32[32,256]{1,0:T(8,128)S(1)} fusion(bf16[2,2048,256]{2,1,0:T(8,128)(2,1)} %param.14, bf16[32,8192]{1,0:T(8,128)(2,1)S(1)} %all_gather.6, s32[]{:T(128)S(6)} %select_n.32), kind=kOutput, calls=%fused_computation.14 | convolution fusion | flops 33554432 | bytes 1212420 | tf_op jit(solution)/shard_map/dot_general | solution.py:149
  39.0 0.0 slice-start.1
  39.0 5.1 %fusion.37 = f32[32,2048]{1,0:T(8,128)S(1)} fusion(bf16[2048,2048]{1,0:T(8,128)(2,1)} %param.13, bf16[32,8192]{1,0:T(8,128)(2,1)S(1)} %all_gather.6, s32[]{:T(128)S(6)} %select_n.32), kind=kOutput, calls=%fused_computation.39 | convolution fusion | flops 268435456 | bytes 8781828 | tf_op jit(solution)/shard_map/dot_general | solution.py:148
  44.1 0.0 slice-done
  44.1 0.0 slice-done.1
  44.1 0.0 copy-start.1
  44.1 3.7 %fusion.8 = f32[48,32]{0,1:T(8,128)S(1)} fusion(bf16[32,48,2048]{2,1,0:T(8,128)(2,1)S(1)} %bitcast.53, pred[32,32]{1,0:T(8,128)(4,1)S(1)} %get-tuple-element.21, bf16[32,8192]{1,0:T(8,128)(2,1)S(1)} %all_gather.6, s32[]{:T(128)S(6)} %select_n.33), kind=kOutput, calls=%fused_computation.8 | convolution fusion | flops 201423360 | bytes 6432772 | tf_op jit(solution)/shard_map/omk,lk->oml/dot_general | solution.py:106
  47.8 17.4 %psum.7 = bf16[48,32]{0,1:T(8,128)(2,1)S(1)} all-reduce(f32[48,32]{0,1:T(8,128)S(1)} %fusion.8), channel_id=1, replica_groups=mesh['groups'=2,'bank'=4,'tensor'=4] {'tensor'}, use_global_device_ids=true, to_apply=%region_3.4 | all-reduce | flops 1536 | bytes 9216 | tf_op jit(solution)/shard_map/psum | solution.py:110
  65.2 0.1 fusion.56
  65.3 0.1 copy.27
  65.4 0.1 copy.28
  65.5 0.1 copy.26
  65.6 0.2 fusion.58
  65.8 0.2 fusion.57
  66.0 0.0 copy-done
  66.0 0.5 convolution_bitcast_fusion
  66.5 0.8 maximum_add_fusion
  67.3 0.0 reduce-scatter.2.cloned.1.call-update
  67.3 0.0 copy-done.1
  67.3 0.1 multiply_cosine_fusion
  67.4 18.3 %reduce-scatter.2.cloned.1.call-done = f32[8,2560]{1,0:T(8,128)} async-done(((f32[32,2560]{1,0:T(8,128)}), f32[8,2560]{1,0:T(8,128)}) %reduce-scatter.2.cloned.1.call-update) | async-done | bytes 81936 | tf_op jit(solution)/shard_map/reduce_scatter | solution.py:145
  85.7 0.0 copy-start.2
  85.7 1.0 slice_bitcast_fusion
  86.7 0.1 subtract_convert_fusion
  86.8 0.9 slice_bitcast_fusion.1
  87.7 0.1 subtract_convert_fusion.1
  87.8 0.1 maximum_bitcast_fusion
  87.8 3.5 %select_reduce_fusion = (f32[8,2,8]{2,1,0:T(2,128)S(1)}, f32[8,2,8,1024]{3,2,1,0:T(8,128)S(1)}) fusion(s32[8]{0:T(128)S(1)} %copy-done.1, bf16[8,1024,2,128]{3,2,1,0:T(2,128)(2,1)} %param.20, bf16[8,2,8,64]{3,2,1,0:T(8,128)(2,1)S(1)} %get-tuple-element.24, bf16[8,2,8,64]{3,2,1,0:T(8,128)(2,1)S(1)} %get-tuple-element.25), kind=kOutput, calls=%fused_computation.20 | convolution fusion | flops 34144128 | bytes 4751904 | tf_op jit(solution)/shard_map/bkgd,bpkd->bkgp/dot_general | solution.py:31
  91.4 0.2 fusion.41
  91.6 0.3 fusion.24
  91.9 0.7 fusion.44
  92.6 0.0 copy-done.2
  92.6 0.8 fusion.15
  93.4 0.6 copy.56
  (17 shorter events, 0.1 us)
Async XLA Ops:
  6.5 59.5 %copy-start = (bf16[32,16,2048]{2,1,0:T(8,128)(2,1)S(1)}, bf16[32,16,2048]{2,1,0:T(8,128)(2,1)}, u32[]{:S(2)}) copy-start(bf16[32,16,2048]{2,1,0:T(8,128)(2,1)} %param.16) | copy-start | bytes 6291460
  6.5 79.1 %reduce-scatter.2.cloned.1.call-start = ((), (), s32[]{:S(2)}) async-start(), calls=%async_computation.1 | async-start | bytes 409600 | tf_op jit(solution)/shard_map/reduce_scatter | solution.py:145
  6.5 7.2 %collective-permute-start = (bf16[8,2048]{1,0:T(8,128)(2,1)}, bf16[8,2048]{1,0:T(8,128)(2,1)S(1)}, u32[]{:S(2)}, u32[]{:S(2)}) collective-permute-start(bf16[8,2048]{1,0:T(8,128)(2,1)} %param.11), channel_id=1, source_target_pairs={{0,1},{1,2},{2,3},{3,0},{4,5},{5,6},{6,7},{7,4},{8,9},{9,10},{10,1... | collective-permute-start | bytes 98312 | tf_op jit(solution)/shard_map/ppermute | solution.py:73
  13.7 7.9 %collective-permute-start.1 = (bf16[8,2048]{1,0:T(8,128)(2,1)S(1)}, bf16[8,2048]{1,0:T(8,128)(2,1)S(1)}, u32[]{:S(2)}, u32[]{:S(2)}) collective-permute-start(bf16[8,2048]{1,0:T(8,128)(2,1)S(1)} %collective-permute-done), channel_id=1, source_target_pairs={{0,1},{1,2},{2,3},{3,0},{4,5},{5,6},{6,7},{7,4},{8,9},{9,10},{10,1... | collective-permute-start | bytes 98312 | tf_op jit(solution)/shard_map/ppermute | solution.py:73
  21.6 5.7 %collective-permute-start.2 = (bf16[8,2048]{1,0:T(8,128)(2,1)S(1)}, bf16[8,2048]{1,0:T(8,128)(2,1)S(1)}, u32[]{:S(2)}, u32[]{:S(2)}) collective-permute-start(bf16[8,2048]{1,0:T(8,128)(2,1)S(1)} %collective-permute-done.1), channel_id=1, source_target_pairs={{0,1},{1,2},{2,3},{3,0},{4,5},{5,6},{6,7},{7,4},{8,9},{9,10},{10,1... | collective-permute-start | bytes 98312 | tf_op jit(solution)/shard_map/ppermute | solution.py:73
  37.3 6.8 %slice-start = ((s8[6291456]{0:T(1024)(128)(4,1)}), s8[4194304]{0:T(1024)(128)(4,1)S(1)}, s32[]{:S(2)}) async-start(s8[6291456]{0:T(1024)(128)(4,1)} %bitcast.52), calls=%async_computation.2 | async-start | bytes 8388608
  39.0 5.1 %slice-start.1 = ((s8[6291456]{0:T(1024)(128)(4,1)}), s8[2097152]{0:T(1024)(128)(4,1)S(1)}, s32[]{:S(2)}) async-start(s8[6291456]{0:T(1024)(128)(4,1)} %bitcast.52), calls=%async_computation.3 | async-start | bytes 4194304
  44.1 23.2 %copy-start.1 = (s32[8]{0:T(128)S(1)}, s32[8]{0:T(128)}, u32[]{:S(2)}) copy-start(s32[8]{0:T(128)} %param.19) | copy-start | bytes 100
  85.7 6.9 %copy-start.2 = (bf16[8,1024,2,128]{3,2,1,0:T(2,128)(2,1)S(1)}, bf16[8,1024,2,128]{3,2,1,0:T(2,128)(2,1)}, u32[]{:S(2)}) copy-start(bf16[8,1024,2,128]{3,2,1,0:T(2,128)(2,1)} %param.21) | copy-start | bytes 12582916
Sparse Core Ops, SparseCore 0:
  67.4 18.2 reduce-scatter.1
